TPU v7x, 32 devices: a whole 2x2x4 slice. The times are simulated.
32 devices in a mesh: tok: 32 (over z, y, x, core), head: 1.
Axes of the slice: x: 2, y: 2, z: 4, core: 2. Of those that a mesh axis runs over, the one named last changes fastest.
Arguments:
- queries: bfloat16 [32768, 4096], P('tok', 'head'), may hold values from -6 to 6
- keys: bfloat16 [32768, 4096], P('tok', 'head'), may hold values from -6 to 6
- values: bfloat16 [32768, 4096], P('tok', 'head'), may hold values from -6 to 6
- rates: float32 [8, 32768], P('head', 'tok'), may hold values from 0.02 to 0.2
- w_gate: bfloat16 [8, 512, 512], P('head', 'tok'), may hold values from -0.25 to 0.25
- w_up: bfloat16 [8, 512, 512], P('head', 'tok'), may hold values from -0.25 to 0.25
- w_down: bfloat16 [8, 512, 512], P('head', 'tok'), may hold values from -0.25 to 0.25
- out_gain: float32 [4096], P('head'), may hold values from 0.1 to 1.9
Outputs:
- mixed: bfloat16 [32768, 4096], P('tok', 'head')
All inputs are finite; a program needn't handle non-finite values.
Results may differ from a plain program's by a relative error of at most 0.009.
Values may be sent and summed in bfloat16 or wider, within the bound.
No kernel may reach another device: no remote copies, remote signals or barrier semaphores. Data moves between devices by JAX's collectives and lax.ppermute only.
A program may use at most 192 MiB of HBM per device.

v0:
```python
import functools
import math

import jax
import jax.numpy as jnp
from jax import lax
from jax.experimental import pallas as pl
from jax.experimental.pallas import tpu as pltpu
from jax.sharding import PartitionSpec as P


F32 = jnp.float32
BF16 = jnp.bfloat16


def activate(gate):
    sigma = jax.nn.sigmoid(gate)
    return (gate * sigma, sigma * (1.0 + gate * (1.0 - sigma)))


def apply_heads(inputs, weights):
    return jnp.einsum("thi,hij->thj", inputs, weights, preferred_element_type=F32)


def scaled_columns(updated, norms):
    return (updated * lax.rsqrt(norms + 1e-06)[:, None, :]).astype(BF16)


def query_pass(query_rows, new_gate, new_up, new_down):
    query_gate = apply_heads(query_rows, new_gate)
    query_up = apply_heads(query_rows, new_up)
    query_act, _ = activate(query_gate)
    query_hidden = (query_act * query_up).astype(BF16)
    return apply_heads(query_hidden, new_down)


def plain_shards(queries, keys, values, rates, w_gate, w_up, w_down, out_gain):
    heads = w_gate.shape[0]
    width = w_gate.shape[2]
    rows = keys.shape[0]
    total = rows * lax.axis_size("tok")
    full_gate, full_up, full_down = (
        lax.all_gather(w_gate, "tok", axis=1, tiled=True),
        lax.all_gather(w_up, "tok", axis=1, tiled=True),
        lax.all_gather(w_down, "tok", axis=1, tiled=True),
    )
    key_rows = keys.reshape(rows, heads, width)
    value_rows = values.reshape(rows, heads, width).astype(F32)
    query_rows = queries.reshape(rows, heads, width)
    scale = rates.T / math.sqrt(total)
    gate = apply_heads(key_rows, full_gate)
    up = apply_heads(key_rows, full_up)
    act, slope = activate(gate)
    hidden = (act * up).astype(BF16)
    fitted = apply_heads(hidden, full_down)
    error = (scale[:, :, None] * (fitted - value_rows)).astype(BF16)
    grad_down = jnp.einsum("thi,thj->hij", hidden, error, preferred_element_type=F32)
    back = jnp.einsum("thj,hij->thi", error, full_down, preferred_element_type=F32)
    grad_gate = jnp.einsum(
        "thi,thj->hij", key_rows, (back * up * slope).astype(BF16), preferred_element_type=F32
    )
    grad_up = jnp.einsum("thi,thj->hij", key_rows, (back * act).astype(BF16), preferred_element_type=F32)
    sum_gate, sum_up, sum_down = lax.psum((grad_gate, grad_up, grad_down), "tok")
    updated = [
        full_gate.astype(F32) - sum_gate,
        full_up.astype(F32) - sum_up,
        full_down.astype(F32) - sum_down,
    ]
    new_gate, new_up, new_down = [scaled_columns(item, jnp.sum(item * item, axis=1)) for item in updated]
    applied = query_pass(query_rows, new_gate, new_up, new_down)
    flat = applied.reshape(rows, heads * width)
    square = lax.psum(jnp.sum(flat * flat, axis=1), "head")
    inverse = lax.rsqrt(square / (heads * width * lax.axis_size("head")) + 1e-06)
    return (flat * inverse[:, None] * out_gain[None, :]).astype(BF16)


def masks_of(chips, odd):
    planes = chips // 4
    masks = [4 << bit for bit in reversed(range(planes.bit_length() - 1))]
    return masks + ([1, 2] if odd else [2, 1])


def mask_of(piece, masks):
    value = 0
    for bit, mask in enumerate(masks):
        if piece >> bit & 1:
            value ^= mask
    return value


def flip(array, mask, devices):
    return lax.ppermute(array, "tok", [(i, i ^ mask) for i in range(devices)])


def gather_pieces(own, masks, devices):
    for stage, mask in enumerate(masks):
        got = flip(own, 2 * mask, devices)
        if stage == len(masks) - 1:
            return own, got
        own = jnp.concatenate([own, got], axis=0)


def gather_planes(own, masks, devices):
    own = own[:, None]
    for mask in masks:
        got = flip(own, 2 * mask, devices)
        own = jnp.concatenate([own, got], axis=1)
    return own


def add(a, b):
    return a.astype(F32) + b.astype(F32)


def reduce_pieces(keep, send, masks, devices):
    got = flip(send, 2 * masks[-1], devices)
    for mask in reversed(masks[1:-1]):
        half = keep.shape[0] // 2
        send = add(keep[half:], got[half:]).astype(BF16)
        keep = add(keep[:half], got[:half])
        got = flip(send, 2 * mask, devices)
    keep = add(keep, got)
    got = flip(keep.astype(BF16), 2 * masks[0], devices)
    return keep + jnp.stack([got[1], got[0]]).astype(F32)


def assemble(place_ref, own_ref, got_ref, wide_ref, down_ref, masks):
    pieces, _, rows, width = own_ref.shape
    chip = place_ref[1]
    for piece in range(2 * pieces):
        source = own_ref if piece < pieces else got_ref
        at = pl.multiple_of((chip ^ mask_of(piece, masks)) * rows, rows)
        index = piece % pieces
        wide_ref[pl.ds(at, rows), :width] = source[index, 0]
        wide_ref[pl.ds(at, rows), width:] = source[index, 1]
        down_ref[pl.ds(at, rows), :] = source[index, 2]


def contract_rows(a, b):
    return lax.dot_general(a, b, (((0,), (0,)), ((), ())), preferred_element_type=F32)


def learn_kernel(
    place_ref, k_own, k_got, v_own, v_got, scale_ref, own_ref, got_ref,
    keep_ref, send_ref, wide, down, grad_wide, grad_down, *, head, masks, out_masks, tiles,
):
    step = pl.program_id(0)
    width = down.shape[1]

    @pl.when(step == 0)
    def _():
        assemble(place_ref, own_ref, got_ref, wide, down, masks)
        grad_wide[...] = jnp.zeros_like(grad_wide)
        grad_down[...] = jnp.zeros_like(grad_down)

    def tile(k_ref, v_ref):
        k = k_ref[...]
        both = jnp.dot(k, wide[...], preferred_element_type=F32)
        gate = both[:, :width]
        up = both[:, width:]
        sigma = 1.0 / (1.0 + jnp.exp(-gate))
        act = gate * sigma
        hidden = (act * up).astype(BF16)
        fitted = jnp.dot(hidden, down[...], preferred_element_type=F32)
        scale = scale_ref[:, head : head + 1]
        error = (scale * (fitted - v_ref[...].astype(F32))).astype(BF16)
        grad_down[...] += contract_rows(hidden, error)
        back = lax.dot_general(
            error, down[...], (((1,), (1,)), ((), ())), preferred_element_type=F32
        )
        slope = sigma + act * (1.0 - sigma)
        dgate = (back * up * slope).astype(BF16)
        dup = (back * act).astype(BF16)
        grad_wide[:, :width] += contract_rows(k, dgate)
        grad_wide[:, width:] += contract_rows(k, dup)

    @pl.when(step < tiles)
    def _():
        tile(k_own, v_own)

    @pl.when(step >= tiles)
    def _():
        tile(k_got, v_got)

    @pl.when(step == 2 * tiles - 1)
    def _():
        pieces, _, rows, _ = keep_ref.shape
        chip = place_ref[1]
        for piece in range(2 * pieces):
            target = keep_ref if piece < pieces else send_ref
            at = pl.multiple_of((chip ^ mask_of(piece, out_masks)) * rows, rows)
            index = piece % pieces
            target[index, 0] = grad_wide[pl.ds(at, rows), :width].astype(target.dtype)
            target[index, 1] = grad_wide[pl.ds(at, rows), width:].astype(target.dtype)
            target[index, 2] = grad_down[pl.ds(at, rows), :].astype(target.dtype)


def answer_kernel(
    place_ref, q_own, q_got, own_ref, got_ref, out_own, out_other,
    wide, down, wide_norm, down_norm, *, masks, tiles,
):
    step = pl.program_id(0)
    width = down.shape[1]

    @pl.when(step == 0)
    def _():
        assemble(place_ref, own_ref, got_ref, wide, down, masks)
        first = wide[...].astype(F32)
        wide_norm[...] = lax.rsqrt(jnp.sum(first * first, axis=0, keepdims=True) + 1e-06)
        second = down[...].astype(F32)
        down_norm[...] = lax.rsqrt(jnp.sum(second * second, axis=0, keepdims=True) + 1e-06)

    def tile(q_ref, out_ref):
        both = jnp.dot(q_ref[...], wide[...], preferred_element_type=F32) * wide_norm[...]
        gate = both[:, :width]
        act = gate / (1.0 + jnp.exp(-gate))
        hidden = (act * both[:, width:]).astype(BF16)
        out = jnp.dot(hidden, down[...], preferred_element_type=F32) * down_norm[...]
        out_ref[...] = out.astype(BF16)

    @pl.when(step < tiles)
    def _():
        tile(q_got, out_other)

    @pl.when(step >= tiles)
    def _():
        tile(q_own, out_own)


def norm_kernel(place_ref, *refs, heads):
    own, got, gain_ref, out_ref = refs[:heads], refs[heads : 2 * heads], refs[-2], refs[-1]
    width = own[0].shape[1]
    total = 0.0
    for ref in own + got:
        block = ref[...].astype(F32)
        total = total + jnp.sum(block * block, axis=1, keepdims=True)
    inverse = lax.rsqrt(total / (2 * heads * width) + 1e-06)

    def write(first, second):
        for index, ref in enumerate(first + second):
            at = slice(index * width, (index + 1) * width)
            out_ref[:, at] = (ref[...].astype(F32) * inverse * gain_ref[:, at]).astype(BF16)

    @pl.when(place_ref[0] == 0)
    def _():
        write(own, got)

    @pl.when(place_ref[0] != 0)
    def _():
        write(got, own)


def tile_of(rows, most):
    size = most
    while rows % size:
        size //= 2
    return size


def fast_shards(*arrays):
    return fast_body(*arrays)


def fast_body(queries, keys, values, rates, w_gate, w_up, w_down, out_gain):
    heads, share, width = w_gate.shape
    if heads % 2:
        return plain_shards(queries, keys, values, rates, w_gate, w_up, w_down, out_gain)
    rows = keys.shape[0]
    devices = lax.axis_size("tok")
    chips = devices // 2
    mine = heads // 2
    total = rows * devices
    place = lax.axis_index("tok")
    core = place % 2
    chip = place // 2
    where = jnp.stack([core, chip]).astype(jnp.int32)

    def halves(array, axis, core):
        size = array.shape[axis] // 2
        keep = lax.dynamic_slice_in_dim(array, core * size, size, axis)
        give = lax.dynamic_slice_in_dim(array, (1 - core) * size, size, axis)
        return keep, flip(give, 1, devices)

    stacked = jnp.stack([w_gate, w_up, w_down], axis=1)
    kept, got = halves(stacked, 0, core)
    pair = jnp.where(core == 0, jnp.stack([kept, got], 2), jnp.stack([got, kept], 2))
    chip_rows = pair.reshape(mine, 3, 2 * share, width)

    masks = masks_of(chips, False)
    lead = len(masks) - 2
    late = masks_of(chips, True)
    early = late[:1] + [late[-2]] + late[1:-2] + late[-1:] if lead > 1 else late
    out_masks = [early if 2 * head < mine else late for head in range(mine)]
    planes = []
    groups = [1] * mine if mine < 4 or mine % 2 else [1, 1] + [2] * (mine // 2 - 1)
    head = 0
    for group in groups:
        both = gather_planes(chip_rows[head : head + group], masks[:lead], devices)
        planes += [both[index] for index in range(group)]
        head += group
    weights = [gather_pieces(planes[head], masks[lead:], devices) for head in range(mine)]

    own_rates, got_rates = halves(rates, 0, core)
    scale = jnp.concatenate([own_rates, got_rates], axis=1).T / math.sqrt(total)
    key_got = halves(keys, 1, core)[1]
    value_got = halves(values, 1, core)[1]

    size = tile_of(rows, 512)
    tiles = rows // size
    piece_rows = 2 * share
    half = chips // 2

    def pieces_spec():
        return pl.BlockSpec((half, 3, piece_rows, width), lambda t, s: (0, 0, 0, 0))

    def own_spec(head, late):
        if late:
            return pl.BlockSpec((size, width), lambda t, s: (jnp.maximum(t - tiles, 0), s[0] * mine + head))
        return pl.BlockSpec((size, width), lambda t, s: (jnp.minimum(t, tiles - 1), s[0] * mine + head))

    def got_spec(head, late):
        if late:
            return pl.BlockSpec((size, width), lambda t, s: (jnp.maximum(t - tiles, 0), head))
        return pl.BlockSpec((size, width), lambda t, s: (jnp.minimum(t, tiles - 1), head))

    def learn(head):
        own, got = weights[head]
        pieces = jax.ShapeDtypeStruct((half, 3, piece_rows, width), BF16)
        return pl.pallas_call(
            functools.partial(learn_kernel, head=head, masks=masks, out_masks=out_masks[head], tiles=tiles),
            out_shape=(jax.ShapeDtypeStruct(pieces.shape, F32), pieces),
            grid_spec=pltpu.PrefetchScalarGridSpec(
                num_scalar_prefetch=1,
                grid=(2 * tiles,),
                in_specs=[
                    own_spec(head, False),
                    got_spec(head, True),
                    own_spec(head, False),
                    got_spec(head, True),
                    pl.BlockSpec((size, mine), lambda t, s: (t, 0)),
                    pieces_spec(),
                    pieces_spec(),
                ],
                out_specs=(pieces_spec(), pieces_spec()),
                scratch_shapes=[
                    pltpu.VMEM((width, 2 * width), BF16),
                    pltpu.VMEM((width, width), BF16),
                    pltpu.VMEM((width, 2 * width), F32),
                    pltpu.VMEM((width, width), F32),
                ],
            ),
            compiler_params=pltpu.CompilerParams(dimension_semantics=("arbitrary",)),
            cost_estimate=pl.CostEstimate(
                flops=28 * rows * width * width, transcendentals=4 * rows * width,
                bytes_accessed=8 * rows * width + 12 * width * width,
            ),
        )(where, keys, key_got, values, value_got, scale, own, got)

    def answer(head, own, got):
        side = jax.ShapeDtypeStruct((rows, width), BF16)
        return pl.pallas_call(
            functools.partial(answer_kernel, masks=masks_of(chips, head % 2 == 0), tiles=tiles),
            out_shape=(side, side),
            grid_spec=pltpu.PrefetchScalarGridSpec(
                num_scalar_prefetch=1,
                grid=(2 * tiles,),
                in_specs=[own_spec(head, True), got_spec(head, False), pieces_spec(), pieces_spec()],
                out_specs=(
                    pl.BlockSpec((size, width), lambda t, s: (jnp.maximum(t - tiles, 0), 0)),
                    pl.BlockSpec((size, width), lambda t, s: (jnp.minimum(t, tiles - 1), 0)),
                ),
                scratch_shapes=[
                    pltpu.VMEM((width, 2 * width), BF16),
                    pltpu.VMEM((width, width), BF16),
                    pltpu.VMEM((1, 2 * width), F32),
                    pltpu.VMEM((1, width), F32),
                ],
            ),
            compiler_params=pltpu.CompilerParams(dimension_semantics=("arbitrary",)),
            cost_estimate=pl.CostEstimate(
                flops=12 * rows * width * width, transcendentals=4 * rows * width,
                bytes_accessed=8 * rows * width + 6 * width * width,
            ),
        )(where, queries, query_got, own, got)

    outs_own = []
    outs_got = []
    learned = []
    for head in range(mine):
        learned.append(learn(head))
    core_query = lax.optimization_barrier((core, learned[-1][1]))[0]
    query_got = halves(queries, 1, core_query)[1]
    for head in range(mine):
        keep, send = learned[head]
        summed = reduce_pieces(keep, send, out_masks[head], devices)
        fresh = (planes[head][: summed.shape[0]].astype(F32) - summed).astype(BF16)
        own, got = gather_pieces(fresh, masks_of(chips, head % 2 == 0)[1:], devices)
        out_own, out_other = answer(head, own, got)
        outs_own.append(out_own)
        outs_got.append(flip(out_other, 1, devices))

    size_out = tile_of(rows, 256)
    return pl.pallas_call(
        functools.partial(norm_kernel, heads=mine),
        out_shape=jax.ShapeDtypeStruct((rows, heads * width), BF16),
        grid_spec=pltpu.PrefetchScalarGridSpec(
            num_scalar_prefetch=1,
            grid=(rows // size_out,),
            in_specs=[pl.BlockSpec((size_out, width), lambda t, s: (t, 0))] * (2 * mine)
            + [pl.BlockSpec((1, heads * width), lambda t, s: (0, 0))],
            out_specs=pl.BlockSpec((size_out, heads * width), lambda t, s: (t, 0)),
        ),
        compiler_params=pltpu.CompilerParams(dimension_semantics=("arbitrary",)),
        name="norm",
    )(where, *outs_own, *outs_got, out_gain[None, :])


def solution(mesh):
    in_specs = (
        P("tok", "head"),
        P("tok", "head"),
        P("tok", "head"),
        P("head", "tok"),
        P("head", "tok", None),
        P("head", "tok", None),
        P("head", "tok", None),
        P("head"),
    )
    out_specs = P("tok", "head")
    tok = mesh.shape["tok"]
    fast = mesh.shape["head"] == 1 and tok >= 8 and tok & (tok - 1) == 0
    body = fast_shards if fast else plain_shards
    return jax.shard_map(body, mesh=mesh, in_specs=in_specs, out_specs=out_specs, check_vma=False)
```

profile of v0, /device:TPU:0, one launch (start us, length us, event | category | flops | bytes accessed | tf_op | source)
XLA Modules:
  0.0 319.4 jit_solution(2700956679221691000)
XLA Ops:
  0.0 5.1 %constant_dynamic-slice_fusion.4 = bf16[1024,2048]{1,0:T(8,128)(2,1)} fusion(bf16[1024,4096]{1,0:T(8,128)(2,1)} %v_own.7, s32[]{:T(128)S(6)} %select_n.36), kind=kLoop, calls=%fused_computation.72 | loop fusion | bytes 8388612 | tf_op jit(solution)/shard_map/dynamic_slice | solution.py:281
  9.2 9.7 %collective-permute-done.3 = bf16[4,3,16,512]{3,2,0,1:T(8,128)(2,1)S(1)} collective-permute-done((bf16[4,3,16,512]{3,2,0,1:T(8,128)(2,1)S(1)}, bf16[4,3,16,512]{3,2,0,1:T(8,128)(2,1)S(1)}, u32[]{:S(2)}, u32[]{:S(2)}) %collective-permute-start.3) | collective-permute-done | bytes 196640 | tf_op jit(solution)/shard_map/ppermute | solution.py:92
  18.9 4.0 %collective-permute-start.4 = (bf16[2,1,3,32,512]{4,3,2,1,0:T(8,128)(2,1)S(1)}, bf16[2,1,3,32,512]{4,3,2,1,0:T(8,128)(2,1)S(1)}, u32[]{:S(2)}, u32[]{:S(2)}) collective-permute-start(bf16[2,1,3,32,512]{4,3,2,1,0:T(8,128)(2,1)S(1)} %bitcast.37), channel_id=1, source_target_pairs={{0,16},{1,17},{2,18},{3,19},{4,20},{5,21},{6,22},{7,23},{8,24},{9,... | collective-permute-start | bytes 589832 | tf_op jit(solution)/shard_map/ppermute | solution.py:92
  22.9 9.4 %collective-permute-done.4 = bf16[2,1,3,32,512]{4,3,2,1,0:T(8,128)(2,1)S(1)} collective-permute-done((bf16[2,1,3,32,512]{4,3,2,1,0:T(8,128)(2,1)S(1)}, bf16[2,1,3,32,512]{4,3,2,1,0:T(8,128)(2,1)S(1)}, u32[]{:S(2)}, u32[]{:S(2)}) %collective-permute-start.4) | collective-permute-done | bytes 196640 | tf_op jit(solution)/shard_map/ppermute | solution.py:92
  36.8 8.0 %collective-permute-done.9 = bf16[1,1,3,32,512]{4,3,2,1,0:T(8,128)(2,1)S(1)} collective-permute-done((bf16[1,1,3,32,512]{4,3,2,1,0:T(8,128)(2,1)S(1)}, bf16[1,1,3,32,512]{4,3,2,1,0:T(8,128)(2,1)S(1)}, u32[]{:S(2)}, u32[]{:S(2)}) %collective-permute-start.9) | collective-permute-done | bytes 98336 | tf_op jit(solution)/shard_map/ppermute | solution.py:92
  44.8 3.9 %collective-permute-start.10 = (bf16[1,2,3,32,512]{4,3,2,1,0:T(8,128)(2,1)S(1)}, bf16[1,2,3,32,512]{4,3,2,1,0:T(8,128)(2,1)S(1)}, u32[]{:S(2)}, u32[]{:S(2)}) collective-permute-start(bf16[1,2,3,32,512]{4,3,2,1,0:T(8,128)(2,1)S(1)} %pad_maximum_fusion.15), channel_id=1, source_target_pairs={{0,8},{1,9},{2,10},{3,11},{4,12},{5,13},{6,14},{7,15},{8,0},{9,1},... | collective-permute-start | bytes 589832 | tf_op jit(solution)/shard_map/ppermute | solution.py:92
  56.1 4.8 %collective-permute-done.6 = bf16[4,3,32,512]{3,2,1,0:T(8,128)(2,1)S(1)} collective-permute-done((bf16[4,3,32,512]{3,2,1,0:T(8,128)(2,1)S(1)}, bf16[4,3,32,512]{3,2,1,0:T(8,128)(2,1)S(1)}, u32[]{:S(2)}, u32[]{:S(2)}) %collective-permute-start.6) | collective-permute-done | bytes 393248 | tf_op jit(solution)/shard_map/ppermute | solution.py:92
  79.2 4.7 %collective-permute-done.31 = bf16[4,3,32,512]{3,2,1,0:T(8,128)(2,1)} collective-permute-done((bf16[4,3,32,512]{3,2,1,0:T(8,128)(2,1)S(1)}, bf16[4,3,32,512]{3,2,1,0:T(8,128)(2,1)}, u32[]{:S(2)}, u32[]{:S(2)}) %collective-permute-start.31) | collective-permute-done | bytes 393248 | tf_op jit(solution)/shard_map/ppermute | solution.py:92
  87.1 15.2 %shard_map.82 = (f32[8,3,32,512]{3,2,1,0:T(8,128)}, bf16[8,3,32,512]{3,2,1,0:T(8,128)(2,1)}) custom-call(s32[2]{0:T(128)} %pad_add_fusion.place_ref, bf16[1024,4096]{1,0:T(8,128)(2,1)} %k_own.7, bf16[1024,2048]{1,0:T(8,128)(2,1)} %collective-permute-done.k_got, bf16[1024,4096]{1,0:T(8,128)(2,1)} %v_own.7, bf16[1024,2048]{1,0:T(8,128)(2,1)} %collective-permute-done.1.v_got, ...), custom_call_target="tpu_custom_call" | custom-call | flops 7516192768 | bytes 7340032 | tf_op jit(solution)/shard_map/pallas_call | solution.py:329
  103.9 14.9 %shard_map.83 = (f32[8,3,32,512]{3,2,1,0:T(8,128)}, bf16[8,3,32,512]{3,2,1,0:T(8,128)(2,1)}) custom-call(s32[2]{0:T(128)} %pad_add_fusion.place_ref, bf16[1024,4096]{1,0:T(8,128)(2,1)} %k_own.7, bf16[1024,2048]{1,0:T(8,128)(2,1)} %collective-permute-done.k_got, bf16[1024,4096]{1,0:T(8,128)(2,1)} %v_own.7, bf16[1024,2048]{1,0:T(8,128)(2,1)} %collective-permute-done.1.v_got, ...), custom_call_target="tpu_custom_call" | custom-call | flops 7516192768 | bytes 7340032 | tf_op jit(solution)/shard_map/pallas_call | solution.py:329
  119.3 15.4 %shard_map.85 = (f32[8,3,32,512]{3,2,1,0:T(8,128)}, bf16[8,3,32,512]{3,2,1,0:T(8,128)(2,1)}) custom-call(s32[2]{0:T(128)} %pad_add_fusion.place_ref, bf16[1024,4096]{1,0:T(8,128)(2,1)} %k_own.7, bf16[1024,2048]{1,0:T(8,128)(2,1)} %collective-permute-done.k_got, bf16[1024,4096]{1,0:T(8,128)(2,1)} %v_own.7, bf16[1024,2048]{1,0:T(8,128)(2,1)} %collective-permute-done.1.v_got, ...), custom_call_target="tpu_custom_call" | custom-call | flops 7516192768 | bytes 7340032 | tf_op jit(solution)/shard_map/pallas_call | solution.py:329
  136.2 15.0 %shard_map.87 = (f32[8,3,32,512]{3,2,1,0:T(8,128)}, bf16[8,3,32,512]{3,2,1,0:T(8,128)(2,1)}) custom-call(s32[2]{0:T(128)} %pad_add_fusion.place_ref, bf16[1024,4096]{1,0:T(8,128)(2,1)} %k_own.7, bf16[1024,2048]{1,0:T(8,128)(2,1)} %collective-permute-done.k_got, bf16[1024,4096]{1,0:T(8,128)(2,1)} %v_own.7, bf16[1024,2048]{1,0:T(8,128)(2,1)} %collective-permute-done.1.v_got, ...), custom_call_target="tpu_custom_call" | custom-call | flops 7516192768 | bytes 7340032 | tf_op jit(solution)/shard_map/pallas_call | solution.py:329
  160.3 11.3 %collective-permute-done.33 = bf16[8,3,32,512]{3,2,1,0:T(8,128)(2,1)S(1)} collective-permute-done((bf16[8,3,32,512]{3,2,1,0:T(8,128)(2,1)}, bf16[8,3,32,512]{3,2,1,0:T(8,128)(2,1)S(1)}, u32[]{:S(2)}, u32[]{:S(2)}) %collective-permute-start.33) | collective-permute-done | bytes 786464 | tf_op jit(solution)/shard_map/ppermute | solution.py:92
  178.1 5.9 %collective-permute-done.34 = bf16[4,3,32,512]{3,2,1,0:T(8,128)(2,1)S(1)} collective-permute-done((bf16[4,3,32,512]{3,2,1,0:T(8,128)(2,1)S(1)}, bf16[4,3,32,512]{3,2,1,0:T(8,128)(2,1)S(1)}, u32[]{:S(2)}, u32[]{:S(2)}) %collective-permute-start.34) | collective-permute-done | bytes 393248 | tf_op jit(solution)/shard_map/ppermute | solution.py:92
  194.5 16.3 %collective-permute-done.16 = bf16[2,3,32,512]{3,2,1,0:T(8,128)(2,1)S(1)} collective-permute-done((bf16[2,3,32,512]{3,2,1,0:T(8,128)(2,1)S(1)}, bf16[2,3,32,512]{3,2,1,0:T(8,128)(2,1)S(1)}, u32[]{:S(2)}, u32[]{:S(2)}) %collective-permute-start.16) | collective-permute-done | bytes 196640 | tf_op jit(solution)/shard_map/ppermute | solution.py:92
  211.0 8.0 %collective-permute-done.27 = bf16[2,3,32,512]{3,2,1,0:T(8,128)(2,1)S(1)} collective-permute-done((bf16[2,3,32,512]{3,2,1,0:T(8,128)(2,1)S(1)}, bf16[2,3,32,512]{3,2,1,0:T(8,128)(2,1)S(1)}, u32[]{:S(2)}, u32[]{:S(2)}) %collective-permute-start.27) | collective-permute-done | bytes 196640 | tf_op jit(solution)/shard_map/ppermute | solution.py:92
  221.2 8.3 %collective-permute-done.28 = bf16[2,3,32,512]{3,2,1,0:T(8,128)(2,1)S(1)} collective-permute-done((bf16[2,3,32,512]{3,2,1,0:T(8,128)(2,1)S(1)}, bf16[2,3,32,512]{3,2,1,0:T(8,128)(2,1)S(1)}, u32[]{:S(2)}, u32[]{:S(2)}) %collective-permute-start.28) | collective-permute-done | bytes 196640 | tf_op jit(solution)/shard_map/ppermute | solution.py:92
  233.6 7.0 %collective-permute-done.29 = bf16[4,3,32,512]{3,2,1,0:T(8,128)(2,1)S(1)} collective-permute-done((bf16[4,3,32,512]{3,2,1,0:T(8,128)(2,1)S(1)}, bf16[4,3,32,512]{3,2,1,0:T(8,128)(2,1)S(1)}, u32[]{:S(2)}, u32[]{:S(2)}) %collective-permute-start.29) | collective-permute-done | bytes 393248 | tf_op jit(solution)/shard_map/ppermute | solution.py:92
  245.2 22.6 %collective-permute-done.38 = bf16[4,3,32,512]{3,2,1,0:T(8,128)(2,1)S(1)} collective-permute-done((bf16[4,3,32,512]{3,2,1,0:T(8,128)(2,1)S(1)}, bf16[4,3,32,512]{3,2,1,0:T(8,128)(2,1)S(1)}, u32[]{:S(2)}, u32[]{:S(2)}) %collective-permute-start.38) | collective-permute-done | bytes 393248 | tf_op jit(solution)/shard_map/ppermute | solution.py:92
  270.6 8.6 %shard_map.86 = (bf16[1024,512]{1,0:T(8,128)(2,1)}, bf16[1024,512]{1,0:T(8,128)(2,1)}) custom-call(s32[2]{0:T(128)} %pad_add_fusion.place_ref, bf16[1024,4096]{1,0:T(8,128)(2,1)} %q_own.7, bf16[1024,2048]{1,0:T(8,128)(2,1)} %collective-permute-done.8.q_got, bf16[8,3,32,512]{3,2,1,0:T(8,128)(2,1)} %copy-done, bf16[8,3,32,512]{3,2,1,0:T(8,128)(2,1)} %copy-done.11), custom_call_target="tpu_custom_call" | custom-call | flops 3221225472 | bytes 5767168 | tf_op jit(solution)/shard_map/pallas_call | solution.py:361
  279.2 8.5 %shard_map.84 = (bf16[1024,512]{1,0:T(8,128)(2,1)}, bf16[1024,512]{1,0:T(8,128)(2,1)}) custom-call(s32[2]{0:T(128)} %pad_add_fusion.place_ref, bf16[1024,4096]{1,0:T(8,128)(2,1)} %q_own.7, bf16[1024,2048]{1,0:T(8,128)(2,1)} %collective-permute-done.8.q_got, bf16[8,3,32,512]{3,2,1,0:T(8,128)(2,1)} %copy-done.2, ...), custom_call_target="tpu_custom_call" | custom-call | flops 3221225472 | bytes 5767168 | tf_op jit(solution)/shard_map/pallas_call | solution.py:361
  288.2 8.6 %shard_map.88 = (bf16[1024,512]{1,0:T(8,128)(2,1)}, bf16[1024,512]{1,0:T(8,128)(2,1)}) custom-call(s32[2]{0:T(128)} %pad_add_fusion.place_ref, bf16[1024,4096]{1,0:T(8,128)(2,1)} %q_own.7, bf16[1024,2048]{1,0:T(8,128)(2,1)} %collective-permute-done.8.q_got, bf16[8,3,32,512]{3,2,1,0:T(8,128)(2,1)} %copy-done.3, ...), custom_call_target="tpu_custom_call" | custom-call | flops 3221225472 | bytes 5767168 | tf_op jit(solution)/shard_map/pallas_call | solution.py:361
  296.8 8.8 %shard_map.89 = (bf16[1024,512]{1,0:T(8,128)(2,1)}, bf16[1024,512]{1,0:T(8,128)(2,1)}) custom-call(s32[2]{0:T(128)} %pad_add_fusion.place_ref, bf16[1024,4096]{1,0:T(8,128)(2,1)} %q_own.7, bf16[1024,2048]{1,0:T(8,128)(2,1)} %collective-permute-done.8.q_got, bf16[8,3,32,512]{3,2,1,0:T(8,128)(2,1)} %copy-done.1, ...), custom_call_target="tpu_custom_call" | custom-call | flops 3221225472 | bytes 5767168 | tf_op jit(solution)/shard_map/pallas_call | solution.py:361
  309.6 9.6 %norm.1 = bf16[1024,4096]{1,0:T(8,128)(2,1)} custom-call(s32[2]{0:T(128)} %pad_add_fusion.place_ref, bf16[1024,512]{1,0:T(8,128)(2,1)} %get-tuple-element.26.refs_0_, bf16[1024,512]{1,0:T(8,128)(2,1)} %get-tuple-element.29.refs_1_, bf16[1024,512]{1,0:T(8,128)(2,1)} %get-tuple-element.32.refs_2_, bf16[1024,512]{1,0:T(8,128)(2,1)} %get-tuple-element.34.refs_3_, ...), custom_call_target="tpu_custom_call" | custom-call | tf_op jit(solution)/shard_map/norm/pallas_call | solution.py:403
  (176 shorter events, 85.1 us)
Async XLA Ops:
  5.1 82.0 %collective-permute-start.1 = (bf16[1024,2048]{1,0:T(8,128)(2,1)}, bf16[1024,2048]{1,0:T(8,128)(2,1)}, u32[]{:S(2)}, u32[]{:S(2)}) collective-permute-start(bf16[1024,2048]{1,0:T(8,128)(2,1)} %constant_dynamic-slice_fusion.4), channel_id=1, source_target_pairs={{0,1},{1,0},{2,3},{3,2},{4,5},{5,4},{6,7},{7,6},{8,9},{9,8},{10,11... | collective-permute-start | bytes 12582920 | tf_op jit(solution)/shard_map/ppermute | solution.py:92
  8.5 78.6 %collective-permute-start = (bf16[1024,2048]{1,0:T(8,128)(2,1)}, bf16[1024,2048]{1,0:T(8,128)(2,1)}, u32[]{:S(2)}, u32[]{:S(2)}) collective-permute-start(bf16[1024,2048]{1,0:T(8,128)(2,1)} %constant_dynamic-slice_fusion.5), channel_id=1, source_target_pairs={{0,1},{1,0},{2,3},{3,2},{4,5},{5,4},{6,7},{7,6},{8,9},{9,8},{10,11... | collective-permute-start | bytes 12582920 | tf_op jit(solution)/shard_map/ppermute | solution.py:92
  61.0 25.4 %collective-permute-start.7 = (bf16[8,3,32,512]{3,2,1,0:T(8,128)(2,1)S(1)}, bf16[8,3,32,512]{3,2,1,0:T(8,128)(2,1)}, u32[]{:S(2)}, u32[]{:S(2)}) collective-permute-start(bf16[8,3,32,512]{3,2,1,0:T(8,128)(2,1)S(1)} %pad_maximum_fusion.1.own_ref), channel_id=1, source_target_pairs={{0,2},{1,3},{2,0},{3,1},{4,6},{5,7},{6,4},{7,5},{8,10},{9,11},{10,... | collective-permute-start | bytes 2359304 | tf_op jit(solution)/shard_map/ppermute | solution.py:92
  75.8 28.0 %collective-permute-start.12 = (bf16[8,3,32,512]{3,2,1,0:T(8,128)(2,1)}, bf16[8,3,32,512]{3,2,1,0:T(8,128)(2,1)}, u32[]{:S(2)}, u32[]{:S(2)}) collective-permute-start(bf16[8,3,32,512]{3,2,1,0:T(8,128)(2,1)} %pad_maximum_fusion.2.own_ref), channel_id=1, source_target_pairs={{0,2},{1,3},{2,0},{3,1},{4,6},{5,7},{6,4},{7,5},{8,10},{9,11},{10,... | collective-permute-start | bytes 2359304 | tf_op jit(solution)/shard_map/ppermute | solution.py:92
  83.9 35.4 %collective-permute-start.23 = (bf16[8,3,32,512]{3,2,1,0:T(8,128)(2,1)}, bf16[8,3,32,512]{3,2,1,0:T(8,128)(2,1)}, u32[]{:S(2)}, u32[]{:S(2)}) collective-permute-start(bf16[8,3,32,512]{3,2,1,0:T(8,128)(2,1)} %pad_maximum_fusion.4.own_ref), channel_id=1, source_target_pairs={{0,2},{1,3},{2,0},{3,1},{4,6},{5,7},{6,4},{7,5},{8,10},{9,11},{10,... | collective-permute-start | bytes 2359304 | tf_op jit(solution)/shard_map/ppermute | solution.py:92
  86.5 49.7 %collective-permute-start.32 = (bf16[8,3,32,512]{3,2,1,0:T(8,128)(2,1)S(1)}, bf16[8,3,32,512]{3,2,1,0:T(8,128)(2,1)}, u32[]{:S(2)}, u32[]{:S(2)}) collective-permute-start(bf16[8,3,32,512]{3,2,1,0:T(8,128)(2,1)S(1)} %pad_maximum_fusion.6.own_ref), channel_id=1, source_target_pairs={{0,2},{1,3},{2,0},{3,1},{4,6},{5,7},{6,4},{7,5},{8,10},{9,11},{10,... | collective-permute-start | bytes 2359304 | tf_op jit(solution)/shard_map/ppermute | solution.py:92
  102.3 54.0 %collective-permute-start.40 = (bf16[8,3,32,512]{3,2,1,0:T(8,128)(2,1)}, bf16[8,3,32,512]{3,2,1,0:T(8,128)(2,1)S(1)}, u32[]{:S(2)}, u32[]{:S(2)}) collective-permute-start(bf16[8,3,32,512]{3,2,1,0:T(8,128)(2,1)} %get-tuple-element.22), channel_id=1, source_target_pairs={{0,4},{1,5},{2,6},{3,7},{4,0},{5,1},{6,2},{7,3},{8,12},{9,13},{10,... | collective-permute-start | bytes 2359304 | tf_op jit(solution)/shard_map/ppermute | solution.py:92
  118.8 35.7 %collective-permute-start.13 = (bf16[8,3,32,512]{3,2,1,0:T(8,128)(2,1)}, bf16[8,3,32,512]{3,2,1,0:T(8,128)(2,1)}, u32[]{:S(2)}, u32[]{:S(2)}) collective-permute-start(bf16[8,3,32,512]{3,2,1,0:T(8,128)(2,1)} %get-tuple-element.25), channel_id=1, source_target_pairs={{0,4},{1,5},{2,6},{3,7},{4,0},{5,1},{6,2},{7,3},{8,12},{9,13},{10,... | collective-permute-start | bytes 2359304 | tf_op jit(solution)/shard_map/ppermute | solution.py:92
  134.6 23.6 %collective-permute-start.24 = (bf16[8,3,32,512]{3,2,1,0:T(8,128)(2,1)}, bf16[8,3,32,512]{3,2,1,0:T(8,128)(2,1)S(1)}, u32[]{:S(2)}, u32[]{:S(2)}) collective-permute-start(bf16[8,3,32,512]{3,2,1,0:T(8,128)(2,1)} %get-tuple-element.28), channel_id=1, source_target_pairs={{0,4},{1,5},{2,6},{3,7},{4,0},{5,1},{6,2},{7,3},{8,12},{9,13},{10,... | collective-permute-start | bytes 2359304 | tf_op jit(solution)/shard_map/ppermute | solution.py:92
  151.2 20.4 %collective-permute-start.33 = (bf16[8,3,32,512]{3,2,1,0:T(8,128)(2,1)}, bf16[8,3,32,512]{3,2,1,0:T(8,128)(2,1)S(1)}, u32[]{:S(2)}, u32[]{:S(2)}) collective-permute-start(bf16[8,3,32,512]{3,2,1,0:T(8,128)(2,1)} %get-tuple-element.31), channel_id=1, source_target_pairs={{0,4},{1,5},{2,6},{3,7},{4,0},{5,1},{6,2},{7,3},{8,12},{9,13},{10,... | collective-permute-start | bytes 2359304 | tf_op jit(solution)/shard_map/ppermute | solution.py:92
  154.4 116.1 %collective-permute-start.8 = (bf16[1024,2048]{1,0:T(8,128)(2,1)S(1)}, bf16[1024,2048]{1,0:T(8,128)(2,1)}, u32[]{:S(2)}, u32[]{:S(2)}) collective-permute-start(bf16[1024,2048]{1,0:T(8,128)(2,1)S(1)} %constant_dynamic-slice_fusion), channel_id=1, source_target_pairs={{0,1},{1,0},{2,3},{3,2},{4,5},{5,4},{6,7},{7,6},{8,9},{9,8},{10,11... | collective-permute-start | bytes 12582920 | tf_op jit(solution)/shard_map/ppermute | solution.py:92
  188.1 22.7 %collective-permute-start.16 = (bf16[2,3,32,512]{3,2,1,0:T(8,128)(2,1)S(1)}, bf16[2,3,32,512]{3,2,1,0:T(8,128)(2,1)S(1)}, u32[]{:S(2)}, u32[]{:S(2)}) collective-permute-start(bf16[2,3,32,512]{3,2,1,0:T(8,128)(2,1)S(1)} %fusion.16), channel_id=1, source_target_pairs={{0,16},{1,17},{2,18},{3,19},{4,20},{5,21},{6,22},{7,23},{8,24},{9,... | collective-permute-start | bytes 589832 | tf_op jit(solution)/shard_map/ppermute | solution.py:92
  189.3 30.0 %collective-permute-start.43 = (bf16[2,3,32,512]{3,2,1,0:T(8,128)(2,1)S(1)}, bf16[2,3,32,512]{3,2,1,0:T(8,128)(2,1)S(1)}, u32[]{:S(2)}, u32[]{:S(2)}) collective-permute-start(bf16[2,3,32,512]{3,2,1,0:T(8,128)(2,1)S(1)} %fusion.19), channel_id=1, source_target_pairs={{0,16},{1,17},{2,18},{3,19},{4,20},{5,21},{6,22},{7,23},{8,24},{9,... | collective-permute-start | bytes 589832 | tf_op jit(solution)/shard_map/ppermute | solution.py:92
  191.3 27.7 %collective-permute-start.27 = (bf16[2,3,32,512]{3,2,1,0:T(8,128)(2,1)S(1)}, bf16[2,3,32,512]{3,2,1,0:T(8,128)(2,1)S(1)}, u32[]{:S(2)}, u32[]{:S(2)}) collective-permute-start(bf16[2,3,32,512]{3,2,1,0:T(8,128)(2,1)S(1)} %fusion.17), channel_id=1, source_target_pairs={{0,16},{1,17},{2,18},{3,19},{4,20},{5,21},{6,22},{7,23},{8,24},{9,... | collective-permute-start | bytes 589832 | tf_op jit(solution)/shard_map/ppermute | solution.py:92
  192.6 28.6 %collective-permute-start.36 = (bf16[2,3,32,512]{3,2,1,0:T(8,128)(2,1)S(1)}, bf16[2,3,32,512]{3,2,1,0:T(8,128)(2,1)S(1)}, u32[]{:S(2)}, u32[]{:S(2)}) collective-permute-start(bf16[2,3,32,512]{3,2,1,0:T(8,128)(2,1)S(1)} %fusion.18), channel_id=1, source_target_pairs={{0,16},{1,17},{2,18},{3,19},{4,20},{5,21},{6,22},{7,23},{8,24},{9,... | collective-permute-start | bytes 589832 | tf_op jit(solution)/shard_map/ppermute | solution.py:92
  211.0 19.0 %collective-permute-start.17 = (bf16[2,3,32,512]{3,2,1,0:T(8,128)(2,1)S(1)}, bf16[2,3,32,512]{3,2,1,0:T(8,128)(2,1)S(1)}, u32[]{:S(2)}, u32[]{:S(2)}) collective-permute-start(bf16[2,3,32,512]{3,2,1,0:T(8,128)(2,1)S(1)} %fusion.11), channel_id=1, source_target_pairs={{0,8},{1,9},{2,10},{3,11},{4,12},{5,13},{6,14},{7,15},{8,0},{9,1},... | collective-permute-start | bytes 589832 | tf_op jit(solution)/shard_map/ppermute | solution.py:92
  240.7 28.9 %collective-permute-start.30 = (bf16[8,3,32,512]{3,2,1,0:T(8,128)(2,1)S(1)}, bf16[8,3,32,512]{3,2,1,0:T(8,128)(2,1)S(1)}, u32[]{:S(2)}, u32[]{:S(2)}) collective-permute-start(bf16[8,3,32,512]{3,2,1,0:T(8,128)(2,1)S(1)} %pad_maximum_fusion.5.own_ref), channel_id=1, source_target_pairs={{0,2},{1,3},{2,0},{3,1},{4,6},{5,7},{6,4},{7,5},{8,10},{9,11},{10,... | collective-permute-start | bytes 2359304 | tf_op jit(solution)/shard_map/ppermute | solution.py:92
  240.8 27.0 %collective-permute-start.38 = (bf16[4,3,32,512]{3,2,1,0:T(8,128)(2,1)S(1)}, bf16[4,3,32,512]{3,2,1,0:T(8,128)(2,1)S(1)}, u32[]{:S(2)}, u32[]{:S(2)}) collective-permute-start(bf16[4,3,32,512]{3,2,1,0:T(8,128)(2,1)S(1)} %pad_maximum_fusion.13), channel_id=1, source_target_pairs={{0,2},{1,3},{2,0},{3,1},{4,6},{5,7},{6,4},{7,5},{8,10},{9,11},{10,... | collective-permute-start | bytes 1179656 | tf_op jit(solution)/shard_map/ppermute | solution.py:92
  243.0 25.6 %collective-permute-start.45 = (bf16[4,3,32,512]{3,2,1,0:T(8,128)(2,1)S(1)}, bf16[4,3,32,512]{3,2,1,0:T(8,128)(2,1)S(1)}, u32[]{:S(2)}, u32[]{:S(2)}) collective-permute-start(bf16[4,3,32,512]{3,2,1,0:T(8,128)(2,1)S(1)} %pad_maximum_fusion.14), channel_id=1, source_target_pairs={{0,4},{1,5},{2,6},{3,7},{4,0},{5,1},{6,2},{7,3},{8,12},{9,13},{10,... | collective-permute-start | bytes 1179656 | tf_op jit(solution)/shard_map/ppermute | solution.py:92
  243.4 35.8 %collective-permute-start.19 = (bf16[8,3,32,512]{3,2,1,0:T(8,128)(2,1)S(1)}, bf16[8,3,32,512]{3,2,1,0:T(8,128)(2,1)}, u32[]{:S(2)}, u32[]{:S(2)}) collective-permute-start(bf16[8,3,32,512]{3,2,1,0:T(8,128)(2,1)S(1)} %pad_maximum_fusion.3.own_ref), channel_id=1, source_target_pairs={{0,4},{1,5},{2,6},{3,7},{4,0},{5,1},{6,2},{7,3},{8,12},{9,13},{10,... | collective-permute-start | bytes 2359304 | tf_op jit(solution)/shard_map/ppermute | solution.py:92
  267.9 20.3 %collective-permute-start.39 = (bf16[8,3,32,512]{3,2,1,0:T(8,128)(2,1)S(1)}, bf16[8,3,32,512]{3,2,1,0:T(8,128)(2,1)}, u32[]{:S(2)}, u32[]{:S(2)}) collective-permute-start(bf16[8,3,32,512]{3,2,1,0:T(8,128)(2,1)S(1)} %pad_maximum_fusion.7.own_ref), channel_id=1, source_target_pairs={{0,4},{1,5},{2,6},{3,7},{4,0},{5,1},{6,2},{7,3},{8,12},{9,13},{10,... | collective-permute-start | bytes 2359304 | tf_op jit(solution)/shard_map/ppermute | solution.py:92
  268.6 28.2 %collective-permute-start.46 = (bf16[8,3,32,512]{3,2,1,0:T(8,128)(2,1)S(1)}, bf16[8,3,32,512]{3,2,1,0:T(8,128)(2,1)}, u32[]{:S(2)}, u32[]{:S(2)}) collective-permute-start(bf16[8,3,32,512]{3,2,1,0:T(8,128)(2,1)S(1)} %pad_maximum_fusion.8.own_ref), channel_id=1, source_target_pairs={{0,2},{1,3},{2,0},{3,1},{4,6},{5,7},{6,4},{7,5},{8,10},{9,11},{10,... | collective-permute-start | bytes 2359304 | tf_op jit(solution)/shard_map/ppermute | solution.py:92
  279.1 26.9 %collective-permute-start.48 = (bf16[1024,512]{1,0:T(8,128)(2,1)}, bf16[1024,512]{1,0:T(8,128)(2,1)}, u32[]{:S(2)}, u32[]{:S(2)}) collective-permute-start(bf16[1024,512]{1,0:T(8,128)(2,1)} %get-tuple-element.36), channel_id=1, source_target_pairs={{0,1},{1,0},{2,3},{3,2},{4,5},{5,4},{6,7},{7,6},{8,9},{9,8},{10,11... | collective-permute-start | bytes 3145736 | tf_op jit(solution)/shard_map/ppermute | solution.py:92
  287.7 18.4 %collective-permute-start.47 = (bf16[1024,512]{1,0:T(8,128)(2,1)}, bf16[1024,512]{1,0:T(8,128)(2,1)}, u32[]{:S(2)}, u32[]{:S(2)}) collective-permute-start(bf16[1024,512]{1,0:T(8,128)(2,1)} %get-tuple-element.35), channel_id=1, source_target_pairs={{0,1},{1,0},{2,3},{3,2},{4,5},{5,4},{6,7},{7,6},{8,9},{9,8},{10,11... | collective-permute-start | bytes 3145736 | tf_op jit(solution)/shard_map/ppermute | solution.py:92
  (45 other events, 552.3 us)
where the time goes:
time: 323 us; the launch traced here: 319 us
  waiting for transfers between devices  133 us (41%)
  Pallas kernels  105 us (33%)
  starting transfers between devices  55.4 us (17%)
  local copies, waits for them, and re-layouts  15.5 us (5%)
  other arithmetic  10.2 us (3%)
    ppermute x51, waiting for transfers between devices, flip(): return lax.ppermute(array, 'tok', [(i, i ^ mask) for i in range(devices)])  133 us
    pallas_call x4, Pallas kernels, learn(): pl.pallas_call(functools.partial(learn_kernel, head=head, masks=masks, ou...  60.5 us
    ppermute x51, starting transfers between devices, flip(): return lax.ppermute(array, 'tok', [(i, i ^ mask) for i in range(devices)])  55.4 us
    pallas_call x4, Pallas kernels, answer(): pl.pallas_call(functools.partial(answer_kernel, masks=masks_of(chips, hea...  34.4 us
    dynamic_slice x3, local copies, waits for them, and re-layouts, halves(): give = lax.dynamic_slice_in_dim(array, (1 - core) * size, size, axis)  10 us
    pallas_call x1, Pallas kernels, fast_body(): pl.pallas_call(functools.partial(norm_kernel, heads=mine), out_shape=jax....  9.59 us
  transfers between devices with their start and end apart: 51, of which 19 were waited for; matrix products, arithmetic and copies ran while one was open for 6% of the time, Pallas kernels for 30%

commit v1 on v0

--- a/solution.py
+++ b/solution.py
@@ -153,8 +153,7 @@
         grad_wide[...] = jnp.zeros_like(grad_wide)
         grad_down[...] = jnp.zeros_like(grad_down)
 
-    def tile(k_ref, v_ref):
-        k = k_ref[...]
+    def tile(k, v):
         both = jnp.dot(k, wide[...], preferred_element_type=F32)
         gate = both[:, :width]
         up = both[:, width:]
@@ -163,7 +162,7 @@
         hidden = (act * up).astype(BF16)
         fitted = jnp.dot(hidden, down[...], preferred_element_type=F32)
         scale = scale_ref[:, head : head + 1]
-        error = (scale * (fitted - v_ref[...].astype(F32))).astype(BF16)
+        error = (scale * (fitted - v.astype(F32))).astype(BF16)
         grad_down[...] += contract_rows(hidden, error)
         back = lax.dot_general(
             error, down[...], (((1,), (1,)), ((), ())), preferred_element_type=F32
@@ -174,13 +173,8 @@
         grad_wide[:, :width] += contract_rows(k, dgate)
         grad_wide[:, width:] += contract_rows(k, dup)
 
-    @pl.when(step < tiles)
-    def _():
-        tile(k_own, v_own)
-
-    @pl.when(step >= tiles)
-    def _():
-        tile(k_got, v_got)
+    early = step < tiles
+    tile(jnp.where(early, k_own[...], k_got[...]), jnp.where(early, v_own[...], v_got[...]))
 
     @pl.when(step == 2 * tiles - 1)
     def _():
@@ -210,21 +204,20 @@
         second = down[...].astype(F32)
         down_norm[...] = lax.rsqrt(jnp.sum(second * second, axis=0, keepdims=True) + 1e-06)
 
-    def tile(q_ref, out_ref):
-        both = jnp.dot(q_ref[...], wide[...], preferred_element_type=F32) * wide_norm[...]
-        gate = both[:, :width]
-        act = gate / (1.0 + jnp.exp(-gate))
-        hidden = (act * both[:, width:]).astype(BF16)
-        out = jnp.dot(hidden, down[...], preferred_element_type=F32) * down_norm[...]
-        out_ref[...] = out.astype(BF16)
+    q = jnp.where(step < tiles, q_got[...], q_own[...])
+    both = jnp.dot(q, wide[...], preferred_element_type=F32) * wide_norm[...]
+    gate = both[:, :width]
+    act = gate / (1.0 + jnp.exp(-gate))
+    hidden = (act * both[:, width:]).astype(BF16)
+    out = (jnp.dot(hidden, down[...], preferred_element_type=F32) * down_norm[...]).astype(BF16)
 
     @pl.when(step < tiles)
     def _():
-        tile(q_got, out_other)
+        out_other[...] = out
 
     @pl.when(step >= tiles)
     def _():
-        tile(q_own, out_own)
+        out_own[...] = out
 
 
 def norm_kernel(place_ref, *refs, heads):
@@ -359,7 +352,7 @@
     def answer(head, own, got):
         side = jax.ShapeDtypeStruct((rows, width), BF16)
         return pl.pallas_call(
-            functools.partial(answer_kernel, masks=masks_of(chips, head % 2 == 0), tiles=tiles),
+            functools.partial(answer_kernel, masks=masks_of(chips, (head % 2 == 0) != (2 * head >= mine)), tiles=tiles),
             out_shape=(side, side),
             grid_spec=pltpu.PrefetchScalarGridSpec(
                 num_scalar_prefetch=1,
@@ -394,7 +387,7 @@
         keep, send = learned[head]
         summed = reduce_pieces(keep, send, out_masks[head], devices)
         fresh = (planes[head][: summed.shape[0]].astype(F32) - summed).astype(BF16)
-        own, got = gather_pieces(fresh, masks_of(chips, head % 2 == 0)[1:], devices)
+        own, got = gather_pieces(fresh, masks_of(chips, (head % 2 == 0) != (2 * head >= mine))[1:], devices)
         out_own, out_other = answer(head, own, got)
         outs_own.append(out_own)
         outs_got.append(flip(out_other, 1, devices))

time: 323 us -> 320 us (level); the launches traced: 319 us -> 320 us
  transfers between devices with their start and end apart: 51 -> 51, of which waited for: 19 -> 20; matrix products, arithmetic and copies ran while one was open for 6% -> 6% of each run, Pallas kernels for 30% -> 30%
where the time goes in v1:
time: 320 us
  waiting for transfers between devices  133 us (42%)
  Pallas kernels  104 us (32%)
  starting transfers between devices  56.4 us (18%)
  local copies, waits for them, and re-layouts  15.5 us (5%)
  other arithmetic  10.2 us (3%)
    ppermute x51, waiting for transfers between devices, flip(): return lax.ppermute(array, 'tok', [(i, i ^ mask) for i in range(devices)])  133 us
    pallas_call x4, Pallas kernels, learn(): pl.pallas_call(functools.partial(learn_kernel, head=head, masks=masks, ou...  59.7 us
    ppermute x51, starting transfers between devices, flip(): return lax.ppermute(array, 'tok', [(i, i ^ mask) for i in range(devices)])  56.4 us
    pallas_call x4, Pallas kernels, answer(): pl.pallas_call(functools.partial(answer_kernel, masks=masks_of(chips, (he...  34.8 us
    dynamic_slice x3, local copies, waits for them, and re-layouts, halves(): give = lax.dynamic_slice_in_dim(array, (1 - core) * size, size, axis)  10 us
    pallas_call x1, Pallas kernels, fast_body(): pl.pallas_call(functools.partial(norm_kernel, heads=mine), out_shape=jax....  9.6 us
  transfers between devices with their start and end apart: 51, of which 20 were waited for; matrix products, arithmetic and copies ran while one was open for 6% of the time, Pallas kernels for 30%

profile of v1, /device:TPU:0, one launch (start us, length us, event | category | flops | bytes accessed | tf_op | source)
XLA Modules:
  0.0 319.9 jit_solution(10794959473675654188)
XLA Ops:
  0.0 5.1 %constant_dynamic-slice_fusion.4 = bf16[1024,2048]{1,0:T(8,128)(2,1)} fusion(bf16[1024,4096]{1,0:T(8,128)(2,1)} %v_own.7, s32[]{:T(128)S(6)} %select_n.36), kind=kLoop, calls=%fused_computation.72 | loop fusion | bytes 8388612 | tf_op jit(solution)/shard_map/dynamic_slice | solution.py:274
  9.2 9.7 %collective-permute-done.3 = bf16[4,3,16,512]{3,2,0,1:T(8,128)(2,1)S(1)} collective-permute-done((bf16[4,3,16,512]{3,2,0,1:T(8,128)(2,1)S(1)}, bf16[4,3,16,512]{3,2,0,1:T(8,128)(2,1)S(1)}, u32[]{:S(2)}, u32[]{:S(2)}) %collective-permute-start.3) | collective-permute-done | bytes 196640 | tf_op jit(solution)/shard_map/ppermute | solution.py:92
  18.9 4.0 %collective-permute-start.4 = (bf16[2,1,3,32,512]{4,3,2,1,0:T(8,128)(2,1)S(1)}, bf16[2,1,3,32,512]{4,3,2,1,0:T(8,128)(2,1)S(1)}, u32[]{:S(2)}, u32[]{:S(2)}) collective-permute-start(bf16[2,1,3,32,512]{4,3,2,1,0:T(8,128)(2,1)S(1)} %bitcast.37), channel_id=1, source_target_pairs={{0,16},{1,17},{2,18},{3,19},{4,20},{5,21},{6,22},{7,23},{8,24},{9,... | collective-permute-start | bytes 589832 | tf_op jit(solution)/shard_map/ppermute | solution.py:92
  22.9 9.4 %collective-permute-done.4 = bf16[2,1,3,32,512]{4,3,2,1,0:T(8,128)(2,1)S(1)} collective-permute-done((bf16[2,1,3,32,512]{4,3,2,1,0:T(8,128)(2,1)S(1)}, bf16[2,1,3,32,512]{4,3,2,1,0:T(8,128)(2,1)S(1)}, u32[]{:S(2)}, u32[]{:S(2)}) %collective-permute-start.4) | collective-permute-done | bytes 196640 | tf_op jit(solution)/shard_map/ppermute | solution.py:92
  36.8 8.0 %collective-permute-done.9 = bf16[1,1,3,32,512]{4,3,2,1,0:T(8,128)(2,1)S(1)} collective-permute-done((bf16[1,1,3,32,512]{4,3,2,1,0:T(8,128)(2,1)S(1)}, bf16[1,1,3,32,512]{4,3,2,1,0:T(8,128)(2,1)S(1)}, u32[]{:S(2)}, u32[]{:S(2)}) %collective-permute-start.9) | collective-permute-done | bytes 98336 | tf_op jit(solution)/shard_map/ppermute | solution.py:92
  56.1 4.8 %collective-permute-done.6 = bf16[4,3,32,512]{3,2,1,0:T(8,128)(2,1)S(1)} collective-permute-done((bf16[4,3,32,512]{3,2,1,0:T(8,128)(2,1)S(1)}, bf16[4,3,32,512]{3,2,1,0:T(8,128)(2,1)S(1)}, u32[]{:S(2)}, u32[]{:S(2)}) %collective-permute-start.6) | collective-permute-done | bytes 393248 | tf_op jit(solution)/shard_map/ppermute | solution.py:92
  79.2 4.7 %collective-permute-done.31 = bf16[4,3,32,512]{3,2,1,0:T(8,128)(2,1)} collective-permute-done((bf16[4,3,32,512]{3,2,1,0:T(8,128)(2,1)S(1)}, bf16[4,3,32,512]{3,2,1,0:T(8,128)(2,1)}, u32[]{:S(2)}, u32[]{:S(2)}) %collective-permute-start.31) | collective-permute-done | bytes 393248 | tf_op jit(solution)/shard_map/ppermute | solution.py:92
  87.1 15.1 %shard_map.82 = (f32[8,3,32,512]{3,2,1,0:T(8,128)}, bf16[8,3,32,512]{3,2,1,0:T(8,128)(2,1)}) custom-call(s32[2]{0:T(128)} %pad_add_fusion.place_ref, bf16[1024,4096]{1,0:T(8,128)(2,1)} %k_own.7, bf16[1024,2048]{1,0:T(8,128)(2,1)} %collective-permute-done.k_got, bf16[1024,4096]{1,0:T(8,128)(2,1)} %v_own.7, bf16[1024,2048]{1,0:T(8,128)(2,1)} %collective-permute-done.1.v_got, ...), custom_call_target="tpu_custom_call" | custom-call | flops 7516192768 | bytes 7340032 | tf_op jit(solution)/shard_map/pallas_call | solution.py:322
  103.7 14.9 %shard_map.83 = (f32[8,3,32,512]{3,2,1,0:T(8,128)}, bf16[8,3,32,512]{3,2,1,0:T(8,128)(2,1)}) custom-call(s32[2]{0:T(128)} %pad_add_fusion.place_ref, bf16[1024,4096]{1,0:T(8,128)(2,1)} %k_own.7, bf16[1024,2048]{1,0:T(8,128)(2,1)} %collective-permute-done.k_got, bf16[1024,4096]{1,0:T(8,128)(2,1)} %v_own.7, bf16[1024,2048]{1,0:T(8,128)(2,1)} %collective-permute-done.1.v_got, ...), custom_call_target="tpu_custom_call" | custom-call | flops 7516192768 | bytes 7340032 | tf_op jit(solution)/shard_map/pallas_call | solution.py:322
  119.1 14.8 %shard_map.85 = (f32[8,3,32,512]{3,2,1,0:T(8,128)}, bf16[8,3,32,512]{3,2,1,0:T(8,128)(2,1)}) custom-call(s32[2]{0:T(128)} %pad_add_fusion.place_ref, bf16[1024,4096]{1,0:T(8,128)(2,1)} %k_own.7, bf16[1024,2048]{1,0:T(8,128)(2,1)} %collective-permute-done.k_got, bf16[1024,4096]{1,0:T(8,128)(2,1)} %v_own.7, bf16[1024,2048]{1,0:T(8,128)(2,1)} %collective-permute-done.1.v_got, ...), custom_call_target="tpu_custom_call" | custom-call | flops 7516192768 | bytes 7340032 | tf_op jit(solution)/shard_map/pallas_call | solution.py:322
  135.5 14.8 %shard_map.87 = (f32[8,3,32,512]{3,2,1,0:T(8,128)}, bf16[8,3,32,512]{3,2,1,0:T(8,128)(2,1)}) custom-call(s32[2]{0:T(128)} %pad_add_fusion.place_ref, bf16[1024,4096]{1,0:T(8,128)(2,1)} %k_own.7, bf16[1024,2048]{1,0:T(8,128)(2,1)} %collective-permute-done.k_got, bf16[1024,4096]{1,0:T(8,128)(2,1)} %v_own.7, bf16[1024,2048]{1,0:T(8,128)(2,1)} %collective-permute-done.1.v_got, ...), custom_call_target="tpu_custom_call" | custom-call | flops 7516192768 | bytes 7340032 | tf_op jit(solution)/shard_map/pallas_call | solution.py:322
  159.4 12.1 %collective-permute-done.33 = bf16[8,3,32,512]{3,2,1,0:T(8,128)(2,1)S(1)} collective-permute-done((bf16[8,3,32,512]{3,2,1,0:T(8,128)(2,1)}, bf16[8,3,32,512]{3,2,1,0:T(8,128)(2,1)S(1)}, u32[]{:S(2)}, u32[]{:S(2)}) %collective-permute-start.33) | collective-permute-done | bytes 786464 | tf_op jit(solution)/shard_map/ppermute | solution.py:92
  177.2 6.7 %collective-permute-done.34 = bf16[4,3,32,512]{3,2,1,0:T(8,128)(2,1)S(1)} collective-permute-done((bf16[4,3,32,512]{3,2,1,0:T(8,128)(2,1)S(1)}, bf16[4,3,32,512]{3,2,1,0:T(8,128)(2,1)S(1)}, u32[]{:S(2)}, u32[]{:S(2)}) %collective-permute-start.34) | collective-permute-done | bytes 393248 | tf_op jit(solution)/shard_map/ppermute | solution.py:92
  194.4 16.3 %collective-permute-done.16 = bf16[2,3,32,512]{3,2,1,0:T(8,128)(2,1)S(1)} collective-permute-done((bf16[2,3,32,512]{3,2,1,0:T(8,128)(2,1)S(1)}, bf16[2,3,32,512]{3,2,1,0:T(8,128)(2,1)S(1)}, u32[]{:S(2)}, u32[]{:S(2)}) %collective-permute-start.16) | collective-permute-done | bytes 196640 | tf_op jit(solution)/shard_map/ppermute | solution.py:92
  211.0 8.0 %collective-permute-done.27 = bf16[2,3,32,512]{3,2,1,0:T(8,128)(2,1)S(1)} collective-permute-done((bf16[2,3,32,512]{3,2,1,0:T(8,128)(2,1)S(1)}, bf16[2,3,32,512]{3,2,1,0:T(8,128)(2,1)S(1)}, u32[]{:S(2)}, u32[]{:S(2)}) %collective-permute-start.27) | collective-permute-done | bytes 196640 | tf_op jit(solution)/shard_map/ppermute | solution.py:92
  221.1 8.3 %collective-permute-done.28 = bf16[2,3,32,512]{3,2,1,0:T(8,128)(2,1)S(1)} collective-permute-done((bf16[2,3,32,512]{3,2,1,0:T(8,128)(2,1)S(1)}, bf16[2,3,32,512]{3,2,1,0:T(8,128)(2,1)S(1)}, u32[]{:S(2)}, u32[]{:S(2)}) %collective-permute-start.28) | collective-permute-done | bytes 196640 | tf_op jit(solution)/shard_map/ppermute | solution.py:92
  233.5 7.1 %collective-permute-done.29 = bf16[4,3,32,512]{3,2,1,0:T(8,128)(2,1)S(1)} collective-permute-done((bf16[4,3,32,512]{3,2,1,0:T(8,128)(2,1)S(1)}, bf16[4,3,32,512]{3,2,1,0:T(8,128)(2,1)S(1)}, u32[]{:S(2)}, u32[]{:S(2)}) %collective-permute-start.29) | collective-permute-done | bytes 393248 | tf_op jit(solution)/shard_map/ppermute | solution.py:92
  245.2 7.7 %collective-permute-done.38 = bf16[4,3,32,512]{3,2,1,0:T(8,128)(2,1)S(1)} collective-permute-done((bf16[4,3,32,512]{3,2,1,0:T(8,128)(2,1)S(1)}, bf16[4,3,32,512]{3,2,1,0:T(8,128)(2,1)S(1)}, u32[]{:S(2)}, u32[]{:S(2)}) %collective-permute-start.38) | collective-permute-done | bytes 393248 | tf_op jit(solution)/shard_map/ppermute | solution.py:92
  255.0 14.6 %collective-permute-done.45 = bf16[4,3,32,512]{3,2,1,0:T(8,128)(2,1)S(1)} collective-permute-done((bf16[4,3,32,512]{3,2,1,0:T(8,128)(2,1)S(1)}, bf16[4,3,32,512]{3,2,1,0:T(8,128)(2,1)S(1)}, u32[]{:S(2)}, u32[]{:S(2)}) %collective-permute-start.45) | collective-permute-done | bytes 393248 | tf_op jit(solution)/shard_map/ppermute | solution.py:92
  270.9 8.7 %shard_map.86 = (bf16[1024,512]{1,0:T(8,128)(2,1)}, bf16[1024,512]{1,0:T(8,128)(2,1)}) custom-call(s32[2]{0:T(128)} %pad_add_fusion.place_ref, bf16[1024,4096]{1,0:T(8,128)(2,1)} %q_own.7, bf16[1024,2048]{1,0:T(8,128)(2,1)} %collective-permute-done.8.q_got, bf16[8,3,32,512]{3,2,1,0:T(8,128)(2,1)} %copy-done, bf16[8,3,32,512]{3,2,1,0:T(8,128)(2,1)} %copy-done.11), custom_call_target="tpu_custom_call" | custom-call | flops 3221225472 | bytes 5767168 | tf_op jit(solution)/shard_map/pallas_call | solution.py:354
  279.7 8.7 %shard_map.84 = (bf16[1024,512]{1,0:T(8,128)(2,1)}, bf16[1024,512]{1,0:T(8,128)(2,1)}) custom-call(s32[2]{0:T(128)} %pad_add_fusion.place_ref, bf16[1024,4096]{1,0:T(8,128)(2,1)} %q_own.7, bf16[1024,2048]{1,0:T(8,128)(2,1)} %collective-permute-done.8.q_got, bf16[8,3,32,512]{3,2,1,0:T(8,128)(2,1)} %copy-done.2, ...), custom_call_target="tpu_custom_call" | custom-call | flops 3221225472 | bytes 5767168 | tf_op jit(solution)/shard_map/pallas_call | solution.py:354
  288.9 8.7 %shard_map.88 = (bf16[1024,512]{1,0:T(8,128)(2,1)}, bf16[1024,512]{1,0:T(8,128)(2,1)}) custom-call(s32[2]{0:T(128)} %pad_add_fusion.place_ref, bf16[1024,4096]{1,0:T(8,128)(2,1)} %q_own.7, bf16[1024,2048]{1,0:T(8,128)(2,1)} %collective-permute-done.8.q_got, bf16[8,3,32,512]{3,2,1,0:T(8,128)(2,1)} %copy-done.3, ...), custom_call_target="tpu_custom_call" | custom-call | flops 3221225472 | bytes 5767168 | tf_op jit(solution)/shard_map/pallas_call | solution.py:354
  297.6 8.7 %shard_map.89 = (bf16[1024,512]{1,0:T(8,128)(2,1)}, bf16[1024,512]{1,0:T(8,128)(2,1)}) custom-call(s32[2]{0:T(128)} %pad_add_fusion.place_ref, bf16[1024,4096]{1,0:T(8,128)(2,1)} %q_own.7, bf16[1024,2048]{1,0:T(8,128)(2,1)} %collective-permute-done.8.q_got, bf16[8,3,32,512]{3,2,1,0:T(8,128)(2,1)} %copy-done.1, ...), custom_call_target="tpu_custom_call" | custom-call | flops 3221225472 | bytes 5767168 | tf_op jit(solution)/shard_map/pallas_call | solution.py:354
  310.3 9.6 %norm.1 = bf16[1024,4096]{1,0:T(8,128)(2,1)} custom-call(s32[2]{0:T(128)} %pad_add_fusion.place_ref, bf16[1024,512]{1,0:T(8,128)(2,1)} %get-tuple-element.26.refs_0_, bf16[1024,512]{1,0:T(8,128)(2,1)} %get-tuple-element.29.refs_1_, bf16[1024,512]{1,0:T(8,128)(2,1)} %get-tuple-element.32.refs_2_, bf16[1024,512]{1,0:T(8,128)(2,1)} %get-tuple-element.34.refs_3_, ...), custom_call_target="tpu_custom_call" | custom-call | tf_op jit(solution)/shard_map/norm/pallas_call | solution.py:396
  (176 shorter events, 88.9 us)
Async XLA Ops:
  5.1 82.0 %collective-permute-start.1 = (bf16[1024,2048]{1,0:T(8,128)(2,1)}, bf16[1024,2048]{1,0:T(8,128)(2,1)}, u32[]{:S(2)}, u32[]{:S(2)}) collective-permute-start(bf16[1024,2048]{1,0:T(8,128)(2,1)} %constant_dynamic-slice_fusion.4), channel_id=1, source_target_pairs={{0,1},{1,0},{2,3},{3,2},{4,5},{5,4},{6,7},{7,6},{8,9},{9,8},{10,11... | collective-permute-start | bytes 12582920 | tf_op jit(solution)/shard_map/ppermute | solution.py:92
  8.5 78.6 %collective-permute-start = (bf16[1024,2048]{1,0:T(8,128)(2,1)}, bf16[1024,2048]{1,0:T(8,128)(2,1)}, u32[]{:S(2)}, u32[]{:S(2)}) collective-permute-start(bf16[1024,2048]{1,0:T(8,128)(2,1)} %constant_dynamic-slice_fusion.5), channel_id=1, source_target_pairs={{0,1},{1,0},{2,3},{3,2},{4,5},{5,4},{6,7},{7,6},{8,9},{9,8},{10,11... | collective-permute-start | bytes 12582920 | tf_op jit(solution)/shard_map/ppermute | solution.py:92
  61.0 25.4 %collective-permute-start.7 = (bf16[8,3,32,512]{3,2,1,0:T(8,128)(2,1)S(1)}, bf16[8,3,32,512]{3,2,1,0:T(8,128)(2,1)}, u32[]{:S(2)}, u32[]{:S(2)}) collective-permute-start(bf16[8,3,32,512]{3,2,1,0:T(8,128)(2,1)S(1)} %pad_maximum_fusion.1.own_ref), channel_id=1, source_target_pairs={{0,2},{1,3},{2,0},{3,1},{4,6},{5,7},{6,4},{7,5},{8,10},{9,11},{10,... | collective-permute-start | bytes 2359304 | tf_op jit(solution)/shard_map/ppermute | solution.py:92
  75.8 27.9 %collective-permute-start.12 = (bf16[8,3,32,512]{3,2,1,0:T(8,128)(2,1)}, bf16[8,3,32,512]{3,2,1,0:T(8,128)(2,1)}, u32[]{:S(2)}, u32[]{:S(2)}) collective-permute-start(bf16[8,3,32,512]{3,2,1,0:T(8,128)(2,1)} %pad_maximum_fusion.2.own_ref), channel_id=1, source_target_pairs={{0,2},{1,3},{2,0},{3,1},{4,6},{5,7},{6,4},{7,5},{8,10},{9,11},{10,... | collective-permute-start | bytes 2359304 | tf_op jit(solution)/shard_map/ppermute | solution.py:92
  83.9 35.2 %collective-permute-start.23 = (bf16[8,3,32,512]{3,2,1,0:T(8,128)(2,1)}, bf16[8,3,32,512]{3,2,1,0:T(8,128)(2,1)}, u32[]{:S(2)}, u32[]{:S(2)}) collective-permute-start(bf16[8,3,32,512]{3,2,1,0:T(8,128)(2,1)} %pad_maximum_fusion.4.own_ref), channel_id=1, source_target_pairs={{0,2},{1,3},{2,0},{3,1},{4,6},{5,7},{6,4},{7,5},{8,10},{9,11},{10,... | collective-permute-start | bytes 2359304 | tf_op jit(solution)/shard_map/ppermute | solution.py:92
  86.5 49.0 %collective-permute-start.32 = (bf16[8,3,32,512]{3,2,1,0:T(8,128)(2,1)S(1)}, bf16[8,3,32,512]{3,2,1,0:T(8,128)(2,1)}, u32[]{:S(2)}, u32[]{:S(2)}) collective-permute-start(bf16[8,3,32,512]{3,2,1,0:T(8,128)(2,1)S(1)} %pad_maximum_fusion.6.own_ref), channel_id=1, source_target_pairs={{0,2},{1,3},{2,0},{3,1},{4,6},{5,7},{6,4},{7,5},{8,10},{9,11},{10,... | collective-permute-start | bytes 2359304 | tf_op jit(solution)/shard_map/ppermute | solution.py:92
  102.2 53.2 %collective-permute-start.40 = (bf16[8,3,32,512]{3,2,1,0:T(8,128)(2,1)}, bf16[8,3,32,512]{3,2,1,0:T(8,128)(2,1)S(1)}, u32[]{:S(2)}, u32[]{:S(2)}) collective-permute-start(bf16[8,3,32,512]{3,2,1,0:T(8,128)(2,1)} %get-tuple-element.22), channel_id=1, source_target_pairs={{0,4},{1,5},{2,6},{3,7},{4,0},{5,1},{6,2},{7,3},{8,12},{9,13},{10,... | collective-permute-start | bytes 2359304 | tf_op jit(solution)/shard_map/ppermute | solution.py:92
  118.6 35.0 %collective-permute-start.13 = (bf16[8,3,32,512]{3,2,1,0:T(8,128)(2,1)}, bf16[8,3,32,512]{3,2,1,0:T(8,128)(2,1)}, u32[]{:S(2)}, u32[]{:S(2)}) collective-permute-start(bf16[8,3,32,512]{3,2,1,0:T(8,128)(2,1)} %get-tuple-element.25), channel_id=1, source_target_pairs={{0,4},{1,5},{2,6},{3,7},{4,0},{5,1},{6,2},{7,3},{8,12},{9,13},{10,... | collective-permute-start | bytes 2359304 | tf_op jit(solution)/shard_map/ppermute | solution.py:92
  133.9 23.3 %collective-permute-start.24 = (bf16[8,3,32,512]{3,2,1,0:T(8,128)(2,1)}, bf16[8,3,32,512]{3,2,1,0:T(8,128)(2,1)S(1)}, u32[]{:S(2)}, u32[]{:S(2)}) collective-permute-start(bf16[8,3,32,512]{3,2,1,0:T(8,128)(2,1)} %get-tuple-element.28), channel_id=1, source_target_pairs={{0,4},{1,5},{2,6},{3,7},{4,0},{5,1},{6,2},{7,3},{8,12},{9,13},{10,... | collective-permute-start | bytes 2359304 | tf_op jit(solution)/shard_map/ppermute | solution.py:92
  150.3 21.2 %collective-permute-start.33 = (bf16[8,3,32,512]{3,2,1,0:T(8,128)(2,1)}, bf16[8,3,32,512]{3,2,1,0:T(8,128)(2,1)S(1)}, u32[]{:S(2)}, u32[]{:S(2)}) collective-permute-start(bf16[8,3,32,512]{3,2,1,0:T(8,128)(2,1)} %get-tuple-element.31), channel_id=1, source_target_pairs={{0,4},{1,5},{2,6},{3,7},{4,0},{5,1},{6,2},{7,3},{8,12},{9,13},{10,... | collective-permute-start | bytes 2359304 | tf_op jit(solution)/shard_map/ppermute | solution.py:92
  153.5 117.4 %collective-permute-start.8 = (bf16[1024,2048]{1,0:T(8,128)(2,1)S(1)}, bf16[1024,2048]{1,0:T(8,128)(2,1)}, u32[]{:S(2)}, u32[]{:S(2)}) collective-permute-start(bf16[1024,2048]{1,0:T(8,128)(2,1)S(1)} %constant_dynamic-slice_fusion), channel_id=1, source_target_pairs={{0,1},{1,0},{2,3},{3,2},{4,5},{5,4},{6,7},{7,6},{8,9},{9,8},{10,11... | collective-permute-start | bytes 12582920 | tf_op jit(solution)/shard_map/ppermute | solution.py:92
  155.7 18.3 %collective-permute-start.41 = (bf16[4,3,32,512]{3,2,1,0:T(8,128)(2,1)S(1)}, bf16[4,3,32,512]{3,2,1,0:T(8,128)(2,1)S(1)}, u32[]{:S(2)}, u32[]{:S(2)}) collective-permute-start(bf16[4,3,32,512]{3,2,1,0:T(8,128)(2,1)S(1)} %get-tuple-element.39), channel_id=1, source_target_pairs={{0,2},{1,3},{2,0},{3,1},{4,6},{5,7},{6,4},{7,5},{8,10},{9,11},{10,... | collective-permute-start | bytes 1179656 | tf_op jit(solution)/shard_map/ppermute | solution.py:92
  188.0 22.7 %collective-permute-start.16 = (bf16[2,3,32,512]{3,2,1,0:T(8,128)(2,1)S(1)}, bf16[2,3,32,512]{3,2,1,0:T(8,128)(2,1)S(1)}, u32[]{:S(2)}, u32[]{:S(2)}) collective-permute-start(bf16[2,3,32,512]{3,2,1,0:T(8,128)(2,1)S(1)} %fusion.16), channel_id=1, source_target_pairs={{0,16},{1,17},{2,18},{3,19},{4,20},{5,21},{6,22},{7,23},{8,24},{9,... | collective-permute-start | bytes 589832 | tf_op jit(solution)/shard_map/ppermute | solution.py:92
  189.2 30.0 %collective-permute-start.43 = (bf16[2,3,32,512]{3,2,1,0:T(8,128)(2,1)S(1)}, bf16[2,3,32,512]{3,2,1,0:T(8,128)(2,1)S(1)}, u32[]{:S(2)}, u32[]{:S(2)}) collective-permute-start(bf16[2,3,32,512]{3,2,1,0:T(8,128)(2,1)S(1)} %fusion.19), channel_id=1, source_target_pairs={{0,16},{1,17},{2,18},{3,19},{4,20},{5,21},{6,22},{7,23},{8,24},{9,... | collective-permute-start | bytes 589832 | tf_op jit(solution)/shard_map/ppermute | solution.py:92
  191.2 27.7 %collective-permute-start.27 = (bf16[2,3,32,512]{3,2,1,0:T(8,128)(2,1)S(1)}, bf16[2,3,32,512]{3,2,1,0:T(8,128)(2,1)S(1)}, u32[]{:S(2)}, u32[]{:S(2)}) collective-permute-start(bf16[2,3,32,512]{3,2,1,0:T(8,128)(2,1)S(1)} %fusion.17), channel_id=1, source_target_pairs={{0,16},{1,17},{2,18},{3,19},{4,20},{5,21},{6,22},{7,23},{8,24},{9,... | collective-permute-start | bytes 589832 | tf_op jit(solution)/shard_map/ppermute | solution.py:92
  192.5 28.6 %collective-permute-start.36 = (bf16[2,3,32,512]{3,2,1,0:T(8,128)(2,1)S(1)}, bf16[2,3,32,512]{3,2,1,0:T(8,128)(2,1)S(1)}, u32[]{:S(2)}, u32[]{:S(2)}) collective-permute-start(bf16[2,3,32,512]{3,2,1,0:T(8,128)(2,1)S(1)} %fusion.18), channel_id=1, source_target_pairs={{0,16},{1,17},{2,18},{3,19},{4,20},{5,21},{6,22},{7,23},{8,24},{9,... | collective-permute-start | bytes 589832 | tf_op jit(solution)/shard_map/ppermute | solution.py:92
  210.9 19.0 %collective-permute-start.17 = (bf16[2,3,32,512]{3,2,1,0:T(8,128)(2,1)S(1)}, bf16[2,3,32,512]{3,2,1,0:T(8,128)(2,1)S(1)}, u32[]{:S(2)}, u32[]{:S(2)}) collective-permute-start(bf16[2,3,32,512]{3,2,1,0:T(8,128)(2,1)S(1)} %fusion.11), channel_id=1, source_target_pairs={{0,8},{1,9},{2,10},{3,11},{4,12},{5,13},{6,14},{7,15},{8,0},{9,1},... | collective-permute-start | bytes 589832 | tf_op jit(solution)/shard_map/ppermute | solution.py:92
  240.7 29.4 %collective-permute-start.30 = (bf16[8,3,32,512]{3,2,1,0:T(8,128)(2,1)S(1)}, bf16[8,3,32,512]{3,2,1,0:T(8,128)(2,1)S(1)}, u32[]{:S(2)}, u32[]{:S(2)}) collective-permute-start(bf16[8,3,32,512]{3,2,1,0:T(8,128)(2,1)S(1)} %pad_maximum_fusion.5.own_ref), channel_id=1, source_target_pairs={{0,2},{1,3},{2,0},{3,1},{4,6},{5,7},{6,4},{7,5},{8,10},{9,11},{10,... | collective-permute-start | bytes 2359304 | tf_op jit(solution)/shard_map/ppermute | solution.py:92
  242.3 27.3 %collective-permute-start.45 = (bf16[4,3,32,512]{3,2,1,0:T(8,128)(2,1)S(1)}, bf16[4,3,32,512]{3,2,1,0:T(8,128)(2,1)S(1)}, u32[]{:S(2)}, u32[]{:S(2)}) collective-permute-start(bf16[4,3,32,512]{3,2,1,0:T(8,128)(2,1)S(1)} %pad_maximum_fusion.14), channel_id=1, source_target_pairs={{0,2},{1,3},{2,0},{3,1},{4,6},{5,7},{6,4},{7,5},{8,10},{9,11},{10,... | collective-permute-start | bytes 1179656 | tf_op jit(solution)/shard_map/ppermute | solution.py:92
  243.3 36.4 %collective-permute-start.19 = (bf16[8,3,32,512]{3,2,1,0:T(8,128)(2,1)S(1)}, bf16[8,3,32,512]{3,2,1,0:T(8,128)(2,1)}, u32[]{:S(2)}, u32[]{:S(2)}) collective-permute-start(bf16[8,3,32,512]{3,2,1,0:T(8,128)(2,1)S(1)} %pad_maximum_fusion.3.own_ref), channel_id=1, source_target_pairs={{0,4},{1,5},{2,6},{3,7},{4,0},{5,1},{6,2},{7,3},{8,12},{9,13},{10,... | collective-permute-start | bytes 2359304 | tf_op jit(solution)/shard_map/ppermute | solution.py:92
  252.9 35.9 %collective-permute-start.39 = (bf16[8,3,32,512]{3,2,1,0:T(8,128)(2,1)S(1)}, bf16[8,3,32,512]{3,2,1,0:T(8,128)(2,1)}, u32[]{:S(2)}, u32[]{:S(2)}) collective-permute-start(bf16[8,3,32,512]{3,2,1,0:T(8,128)(2,1)S(1)} %pad_maximum_fusion.7.own_ref), channel_id=1, source_target_pairs={{0,2},{1,3},{2,0},{3,1},{4,6},{5,7},{6,4},{7,5},{8,10},{9,11},{10,... | collective-permute-start | bytes 2359304 | tf_op jit(solution)/shard_map/ppermute | solution.py:92
  269.7 28.0 %collective-permute-start.46 = (bf16[8,3,32,512]{3,2,1,0:T(8,128)(2,1)S(1)}, bf16[8,3,32,512]{3,2,1,0:T(8,128)(2,1)}, u32[]{:S(2)}, u32[]{:S(2)}) collective-permute-start(bf16[8,3,32,512]{3,2,1,0:T(8,128)(2,1)S(1)} %pad_maximum_fusion.8.own_ref), channel_id=1, source_target_pairs={{0,4},{1,5},{2,6},{3,7},{4,0},{5,1},{6,2},{7,3},{8,12},{9,13},{10,... | collective-permute-start | bytes 2359304 | tf_op jit(solution)/shard_map/ppermute | solution.py:92
  279.6 27.1 %collective-permute-start.48 = (bf16[1024,512]{1,0:T(8,128)(2,1)}, bf16[1024,512]{1,0:T(8,128)(2,1)}, u32[]{:S(2)}, u32[]{:S(2)}) collective-permute-start(bf16[1024,512]{1,0:T(8,128)(2,1)} %get-tuple-element.36), channel_id=1, source_target_pairs={{0,1},{1,0},{2,3},{3,2},{4,5},{5,4},{6,7},{7,6},{8,9},{9,8},{10,11... | collective-permute-start | bytes 3145736 | tf_op jit(solution)/shard_map/ppermute | solution.py:92
  288.4 18.4 %collective-permute-start.47 = (bf16[1024,512]{1,0:T(8,128)(2,1)}, bf16[1024,512]{1,0:T(8,128)(2,1)}, u32[]{:S(2)}, u32[]{:S(2)}) collective-permute-start(bf16[1024,512]{1,0:T(8,128)(2,1)} %get-tuple-element.35), channel_id=1, source_target_pairs={{0,1},{1,0},{2,3},{3,2},{4,5},{5,4},{6,7},{7,6},{8,9},{9,8},{10,11... | collective-permute-start | bytes 3145736 | tf_op jit(solution)/shard_map/ppermute | solution.py:92
  (45 other events, 564.6 us)
